TPU v7x, 32 devices: a whole 2x2x4 slice. The times are simulated.
32 devices in a mesh: gx: 4 (over y, core), gy: 8 (over z, x).
Axes of the slice: x: 2, y: 2, z: 4, core: 2. Of those that a mesh axis runs over, the one named last changes fastest.
Arguments:
- transfer: bfloat16 [512, 75, 128], P(('gx', 'gy')), may hold values from -6 to 6
- positions: float32 [512, 3, 128], P(('gx', 'gy')), may hold values from -4 to 4
- normals: float32 [512, 3, 128], P(('gx', 'gy')), may hold values from -4 to 4
- area: float32 [512, 128], P(('gx', 'gy')), may hold values from 0.06 to 3
- albedo: float32 [512, 3, 128], P(('gx', 'gy')), may hold values from 0.3 to 0.9
- pairs: int32 [512, 40], P(('gx', 'gy')), may hold values from 0 to 511, as said below
- home: int32 [512], replicated, may hold values from 0 to 511, as said below
Outputs:
- bounce_one: bfloat16 [512, 75, 128], P(('gx', 'gy'))
- bounce_two: bfloat16 [512, 75, 128], P(('gx', 'gy'))
- energies: float32 [2], replicated
Inputs may be any that keep to these rules, and one draw needn't show every extreme that they name: `home`: A permutation; the block in slot s is held by device s // 16, devices counted gx major. `pairs`: the first 16 entries of a row name blocks held by the same device as the row's slot, the other 24 name blocks held by other devices. Over the rows of one device, the far entries name at most 2 distinct blocks of any one other device, and exactly 2 of some. Ids may repeat within a row; each entry counts.
All inputs are finite; a program needn't handle non-finite values.
Results may differ from a plain program's by a relative error of at most 0.02.
Values may be sent and summed in bfloat16 or wider, within the bound.
A program may use at most 128 MiB of HBM per device.

v0:
```python
import jax
import jax.numpy as jnp
from jax import lax
from jax.sharding import PartitionSpec as P

COLORS = 3
NEAR = 16
CAP = 2
batch_blocks = 4


def form_tiles(recv_pos, recv_nrm, src_pos, src_nrm, src_area):
    distance = None
    along_p = None
    along_q = None
    for axis_id in range(3):
        gap_vec = src_pos[:, :, axis_id, None, :] - recv_pos[:, None, axis_id, :, None]
        near_term = recv_nrm[:, None, axis_id, :, None] * gap_vec
        far_term = src_nrm[:, :, axis_id, None, :] * gap_vec
        if distance is None:
            distance = gap_vec * gap_vec
            along_p = near_term
            along_q = far_term
        else:
            distance = distance + gap_vec * gap_vec
            along_p = along_p + near_term
            along_q = along_q + far_term
    soft_sq = distance + 1.0
    transfer_factors = (
        jnp.maximum(along_p, 0.0)
        * jnp.maximum(-along_q, 0.0)
        * src_area[:, :, None, :]
        / (jnp.pi * soft_sq * soft_sq)
    )
    return transfer_factors.astype(jnp.bfloat16)


def build_tiles(src_positions, src_normals, src_area, pair_row_list, recv_positions, recv_normals):
    turns = pair_row_list.shape[0] // batch_blocks

    def group_tiles(group_id):
        first_row = group_id * batch_blocks
        picked_rows = lax.dynamic_slice_in_dim(pair_row_list, first_row, batch_blocks, 0)
        recv_pos = lax.dynamic_slice_in_dim(recv_positions, first_row, batch_blocks, 0)
        recv_nrm = lax.dynamic_slice_in_dim(recv_normals, first_row, batch_blocks, 0)
        return form_tiles(
            recv_pos,
            recv_nrm,
            jnp.take(src_positions, picked_rows, axis=0),
            jnp.take(src_normals, picked_rows, axis=0),
            jnp.take(src_area, picked_rows, axis=0),
        )

    return lax.map(group_tiles, jnp.arange(turns, dtype=jnp.int32))


def apply_tiles(source_rows, pair_row_list, tiles):
    turns = tiles.shape[0]
    grouped_rows = pair_row_list.reshape((turns, batch_blocks) + pair_row_list.shape[1:])

    def group_term(operands):
        picked_rows, transfer_factors = operands
        collected_values = jnp.take(source_rows, picked_rows, axis=0)
        return jnp.einsum(
            "wxmy,wxsy->wms", collected_values, transfer_factors, preferred_element_type=jnp.float32
        )

    summed = lax.map(group_term, (grouped_rows, tiles))
    return summed.reshape((pair_row_list.shape[0],) + source_rows.shape[1:])


def apply_albedo(summed, albedo):
    blocks_here, channels, verts = summed.shape
    shaped = summed.reshape(blocks_here, COLORS, channels // COLORS, verts) * albedo[:, :, None, :]
    return shaped.reshape(blocks_here, channels, verts)


def total_energy(local_part):
    return lax.psum(local_part, ("gx", "gy"))


def body(transfer, positions, normals, area, albedo, pairs, home):
    devices_all = lax.axis_size(("gx", "gy"))
    device_id = lax.axis_index(("gx", "gy"))
    per_device = transfer.shape[0]
    slot_ids = jnp.take(home, pairs, axis=0)
    near_rows = slot_ids[:, :NEAR] - device_id * per_device
    distant_slot_ids = slot_ids[:, NEAR:]
    owner_dev = distant_slot_ids // per_device
    flat_need = (
        jnp.zeros((devices_all * per_device,), jnp.int32).at[distant_slot_ids.reshape(-1)].max(1)
    )
    needed = flat_need.reshape(devices_all, per_device)
    rank_in_owner = jnp.cumsum(needed, axis=1) - 1
    picked = (
        (needed[:, :, None] == 1)
        & (rank_in_owner[:, :, None] == jnp.arange(CAP, dtype=jnp.int32)[None, None, :])
    ).astype(jnp.int32)
    filled = jnp.sum(picked, axis=1)
    request_list = jnp.sum(
        picked * jnp.arange(per_device, dtype=jnp.int32)[None, :, None], axis=1
    ) + per_device * (1 - filled)
    far_rows = owner_dev * CAP + jnp.take(rank_in_owner.reshape(-1), distant_slot_ids)
    incident_radiance = lax.all_to_all(
        request_list, ("gx", "gy"), split_axis=0, concat_axis=0, tiled=True
    )
    is_filled = incident_radiance < per_device
    chosen = jnp.minimum(incident_radiance, per_device - 1)

    def outbound(table):
        collected_values = jnp.take(table, chosen, axis=0)
        retain_mask = is_filled.reshape(is_filled.shape + (1,) * (table.ndim - 1))
        return jnp.where(retain_mask, collected_values, jnp.zeros((), table.dtype))

    def direct_table(table):
        return table.reshape((devices_all * CAP,) + table.shape[2:])

    near_tiles = build_tiles(positions, normals, area, near_rows, positions, normals)
    near_first = apply_tiles(transfer, near_rows, near_tiles)
    exitant_radiance = (outbound(transfer), outbound(positions), outbound(normals), outbound(area))
    arrived = (
        lax.all_to_all(exitant_radiance[0], ("gx", "gy"), split_axis=0, concat_axis=0, tiled=True),
        lax.all_to_all(
            exitant_radiance[1].astype(jnp.bfloat16),
            ("gx", "gy"),
            split_axis=0,
            concat_axis=0,
            tiled=True,
        ).astype(jnp.float32),
        lax.all_to_all(
            exitant_radiance[2].astype(jnp.bfloat16),
            ("gx", "gy"),
            split_axis=0,
            concat_axis=0,
            tiled=True,
        ).astype(jnp.float32),
        lax.all_to_all(
            exitant_radiance[3].astype(jnp.bfloat16),
            ("gx", "gy"),
            split_axis=0,
            concat_axis=0,
            tiled=True,
        ).astype(jnp.float32),
    )
    table_transfer = direct_table(arrived[0])
    table_pos = direct_table(arrived[1])
    table_nrm = direct_table(arrived[2])
    table_area = direct_table(arrived[3])
    far_tiles = build_tiles(table_pos, table_nrm, table_area, far_rows, positions, normals)
    far_first = apply_tiles(table_transfer, far_rows, far_tiles)
    first_bounce = apply_albedo(near_first + far_first, albedo)
    bounce_one = first_bounce.astype(jnp.bfloat16)
    local_one = jnp.sum(area[:, None, :] * first_bounce * first_bounce)
    near_second = apply_tiles(bounce_one, near_rows, near_tiles)
    second_table = direct_table(
        lax.all_to_all(outbound(bounce_one), ("gx", "gy"), split_axis=0, concat_axis=0, tiled=True)
    )
    far_second = apply_tiles(second_table, far_rows, far_tiles)
    second_bounce = apply_albedo(near_second + far_second, albedo)
    bounce_two = second_bounce.astype(jnp.bfloat16)
    local_two = jnp.sum(area[:, None, :] * second_bounce * second_bounce)
    energy_one = total_energy(local_one)
    energy_two = total_energy(local_two)
    inv_count = 1.0 / (devices_all * per_device * transfer.shape[2] * transfer.shape[1])
    energies = jnp.stack([energy_one, energy_two]) * inv_count
    return (bounce_one, bounce_two, energies)


def solution(mesh):
    return jax.shard_map(
        body,
        mesh=mesh,
        in_specs=(
            P(("gx", "gy"), None, None),
            P(("gx", "gy"), None, None),
            P(("gx", "gy"), None, None),
            P(("gx", "gy"), None),
            P(("gx", "gy"), None, None),
            P(("gx", "gy"), None),
            P(),
        ),
        out_specs=(P(("gx", "gy"), None, None), P(("gx", "gy"), None, None), P()),
        check_vma=False,
    )
```

profile of v0, /device:TPU:0, one launch (start us, length us, event | category | flops | bytes accessed | tf_op | source)
XLA Modules:
  0.0 292.2 jit_solution(17152638488114444716)
XLA Ops:
  1.5 4.3 %gather_fusion.10 = s32[640]{0:T(1024)S(1)} fusion(s32[512]{0:T(512)S(1)} %copy-done, s32[1024]{0:T(1024)S(1)} %pad_clamp_fusion.9), kind=kCustom, calls=%fused_computation.14 | custom fusion | bytes 7680 | tf_op jit(solution)/shard_map/jit(_take)/gather | solution.py:86
  11.2 7.3 %all-to-all-start = ((s32[32,1,2]{2,1,0:T(1,128)}), s32[32,1,2]{2,1,0:T(1,128)S(1)}, u32[]{:S(2)}, u32[]{:S(2)}) async-start(s32[32,1,2]{2,1,0:T(1,128)} %copy.220), calls=%async_computation | async-start | bytes 32768 | tf_op jit(solution)/shard_map/all_to_all | solution.py:104
  21.7 38.1 %while.60 = (s32[]{:T(128)}, bf16[4,4,16,128,128]{4,3,2,1,0:T(8,128)(2,1)}, s32[4]{0:T(128)S(1)}, f32[16,3,128]{2,1,0:T(4,128)S(1)}, s32[16,16]{1,0:T(8,128)S(1)...) while((s32[]{:T(128)}, ...), condition=%wide.region_1.3_spmd, body=%wide.region_0.0_spmd.sunk | while | flops 29418888 | bytes 3681183 | solution.py:54
  25.4 5.8 %fusion.115 = bf16[4,4,16,128,128]{4,3,2,1,0:T(8,128)(2,1)} fusion(bf16[4,4,16,128,128]{4,3,2,1,0:T(8,128)(2,1)} %get-tuple-element.810, s32[]{:T(128)} %get-tuple-element.809, f32[4,16,128]{2,1,0:T(8,128)S(1)} %broadcast_select_fusion.11, f32[4,16,128]{2,1,0:T(8,128)S(1)} %bitcast.220, f32[4,16,128]{2,1,0:T(8,128)S(1)} %bitcast.219, ...), kind=kLoop, calls=%fused_computation.42.clone.1 | loop fusion | flops 29360128 | bytes 2339328 | tf_op jit(solution)/shard_map/while/body/jit(dynamic_update_index_in_dim)/dynamic_update_slice | solution.py:54
  35.0 5.8 %fusion.115 = bf16[4,4,16,128,128]{4,3,2,1,0:T(8,128)(2,1)} fusion(bf16[4,4,16,128,128]{4,3,2,1,0:T(8,128)(2,1)} %get-tuple-element.810, s32[]{:T(128)} %get-tuple-element.809, f32[4,16,128]{2,1,0:T(8,128)S(1)} %broadcast_select_fusion.11, f32[4,16,128]{2,1,0:T(8,128)S(1)} %bitcast.220, f32[4,16,128]{2,1,0:T(8,128)S(1)} %bitcast.219, ...), kind=kLoop, calls=%fused_computation.42.clone.1 | loop fusion | flops 29360128 | bytes 2339328 | tf_op jit(solution)/shard_map/while/body/jit(dynamic_update_index_in_dim)/dynamic_update_slice | solution.py:54
  44.5 5.8 %fusion.115 = bf16[4,4,16,128,128]{4,3,2,1,0:T(8,128)(2,1)} fusion(bf16[4,4,16,128,128]{4,3,2,1,0:T(8,128)(2,1)} %get-tuple-element.810, s32[]{:T(128)} %get-tuple-element.809, f32[4,16,128]{2,1,0:T(8,128)S(1)} %broadcast_select_fusion.11, f32[4,16,128]{2,1,0:T(8,128)S(1)} %bitcast.220, f32[4,16,128]{2,1,0:T(8,128)S(1)} %bitcast.219, ...), kind=kLoop, calls=%fused_computation.42.clone.1 | loop fusion | flops 29360128 | bytes 2339328 | tf_op jit(solution)/shard_map/while/body/jit(dynamic_update_index_in_dim)/dynamic_update_slice | solution.py:54
  54.0 5.8 %fusion.115 = bf16[4,4,16,128,128]{4,3,2,1,0:T(8,128)(2,1)} fusion(bf16[4,4,16,128,128]{4,3,2,1,0:T(8,128)(2,1)} %get-tuple-element.810, s32[]{:T(128)} %get-tuple-element.809, f32[4,16,128]{2,1,0:T(8,128)S(1)} %broadcast_select_fusion.11, f32[4,16,128]{2,1,0:T(8,128)S(1)} %bitcast.220, f32[4,16,128]{2,1,0:T(8,128)S(1)} %bitcast.219, ...), kind=kLoop, calls=%fused_computation.42.clone.1 | loop fusion | flops 29360128 | bytes 2339328 | tf_op jit(solution)/shard_map/while/body/jit(dynamic_update_index_in_dim)/dynamic_update_slice | solution.py:54
  60.0 14.0 %while.61 = (s32[]{:T(128)}, f32[4,4,75,128]{3,1,0,2:T(4,128)S(1)}, s32[4,4,16]{2,1,0:T(4,128)S(1)}, bf16[16,75,128]{2,1,0:T(8,128)(2,1)S(1)}, bf16[4,4,16,128,128]{4,3,2,1,0:T(8,128)(2,1)}, /*index=5*/s32[]{:T(128)}) while((s32[]{:T(128)}, f32[4,4,75,128]{3,1,0,2:T(4,128)S(1)}, s32[4,4,16]{2,1,0:T(4,128)S(1)}, ...), condition=%wide.region_3.6_spmd, body=%wide.region_2.5_spmd.sunk | while | flops 157902208 | bytes 6260941 | solution.py:68
  77.6 6.0 %all-to-all-start.4 = ((bf16[32,2,128]{2,1,0:T(2,128)(2,1)}), bf16[32,2,128]{2,1,0:T(2,128)(2,1)S(1)}, u32[]{:S(2)}, u32[]{:S(2)}) async-start(bf16[32,2,128]{2,1,0:T(2,128)(2,1)} %select_convert_fusion), calls=%async_computation.4 | async-start | bytes 32768 | tf_op jit(solution)/shard_map/all_to_all | solution.py:137
  84.5 5.4 %gather_fusion.13 = bf16[64,75,128]{2,0,1:T(8,128)(2,1)S(1)} fusion(bf16[16,75,128]{2,0,1:T(8,128)(2,1)S(1)} %copy-done.1, s32[1024]{0:T(1024)S(1)} %pad_clamp_fusion.7), kind=kCustom, calls=%fused_computation.4.clone | custom fusion | bytes 2457856 | tf_op jit(solution)/shard_map/jit(_take)/gather | solution.py:111
  90.6 5.0 %all-to-all-start.2 = ((bf16[32,2,3,128]{3,1,2,0:T(2,128)(2,1)}), bf16[32,2,3,128]{3,1,2,0:T(2,128)(2,1)S(1)}, u32[]{:S(2)}, u32[]{:S(2)}) async-start(bf16[32,2,3,128]{3,1,2,0:T(2,128)(2,1)} %get-tuple-element.491), calls=%async_computation.2 | async-start | bytes 98304 | tf_op jit(solution)/shard_map/all_to_all | solution.py:123
  98.1 4.7 %all-to-all-done.2 = bf16[32,2,3,128]{3,1,2,0:T(2,128)(2,1)S(1)} async-done(((bf16[32,2,3,128]{3,1,2,0:T(2,128)(2,1)}), bf16[32,2,3,128]{3,1,2,0:T(2,128)(2,1)S(1)}, u32[]{:S(2)}, u32[]{:S(2)}) %all-to-all-start.2) | async-done | bytes 49184 | tf_op jit(solution)/shard_map/all_to_all | solution.py:123
  105.6 7.1 %all-to-all-done.3 = bf16[32,2,3,128]{3,1,2,0:T(2,128)(2,1)S(1)} async-done(((bf16[32,2,3,128]{3,1,2,0:T(2,128)(2,1)}), bf16[32,2,3,128]{3,1,2,0:T(2,128)(2,1)S(1)}, u32[]{:S(2)}, u32[]{:S(2)}) %all-to-all-start.3) | async-done | bytes 49184 | tf_op jit(solution)/shard_map/all_to_all | solution.py:130
  115.8 43.3 %while.62 = (s32[]{:T(128)}, bf16[4,4,24,128,128]{4,3,2,1,0:T(8,128)(2,1)}, s32[4]{0:T(128)S(1)}, f32[16,3,128]{2,0,1:T(8,128)S(1)}, s32[16,24]{1,0:T(8,128)S(1)...) while((s32[]{:T(128)}, ...), condition=%wide.region_9.14_spmd, body=%wide.region_8.13_spmd.sunk | while | flops 44127816 | bytes 5500943 | solution.py:54
  119.4 7.2 %fusion.119 = bf16[4,4,24,128,128]{4,3,2,1,0:T(8,128)(2,1)} fusion(bf16[4,4,24,128,128]{4,3,2,1,0:T(8,128)(2,1)} %get-tuple-element.869, s32[]{:T(128)} %get-tuple-element.868, f32[4,24,128]{2,1,0:T(8,128)S(1)} %broadcast_select_fusion.13, f32[4,24,128]{2,1,0:T(8,128)S(1)} %get-tuple-element.763, f32[4,24,128]{2,1,0:T(8,128)S(1)} %get-tuple-element.764, ...), kind=kLoop, calls=%fused_computation.92.clone.1 | loop fusion | flops 44040192 | bytes 3502592 | tf_op jit(solution)/shard_map/while/body/jit(dynamic_update_index_in_dim)/dynamic_update_slice | solution.py:54
  130.2 7.2 %fusion.119 = bf16[4,4,24,128,128]{4,3,2,1,0:T(8,128)(2,1)} fusion(bf16[4,4,24,128,128]{4,3,2,1,0:T(8,128)(2,1)} %get-tuple-element.869, s32[]{:T(128)} %get-tuple-element.868, f32[4,24,128]{2,1,0:T(8,128)S(1)} %broadcast_select_fusion.13, f32[4,24,128]{2,1,0:T(8,128)S(1)} %get-tuple-element.763, f32[4,24,128]{2,1,0:T(8,128)S(1)} %get-tuple-element.764, ...), kind=kLoop, calls=%fused_computation.92.clone.1 | loop fusion | flops 44040192 | bytes 3502592 | tf_op jit(solution)/shard_map/while/body/jit(dynamic_update_index_in_dim)/dynamic_update_slice | solution.py:54
  141.0 7.2 %fusion.119 = bf16[4,4,24,128,128]{4,3,2,1,0:T(8,128)(2,1)} fusion(bf16[4,4,24,128,128]{4,3,2,1,0:T(8,128)(2,1)} %get-tuple-element.869, s32[]{:T(128)} %get-tuple-element.868, f32[4,24,128]{2,1,0:T(8,128)S(1)} %broadcast_select_fusion.13, f32[4,24,128]{2,1,0:T(8,128)S(1)} %get-tuple-element.763, f32[4,24,128]{2,1,0:T(8,128)S(1)} %get-tuple-element.764, ...), kind=kLoop, calls=%fused_computation.92.clone.1 | loop fusion | flops 44040192 | bytes 3502592 | tf_op jit(solution)/shard_map/while/body/jit(dynamic_update_index_in_dim)/dynamic_update_slice | solution.py:54
  151.9 7.2 %fusion.119 = bf16[4,4,24,128,128]{4,3,2,1,0:T(8,128)(2,1)} fusion(bf16[4,4,24,128,128]{4,3,2,1,0:T(8,128)(2,1)} %get-tuple-element.869, s32[]{:T(128)} %get-tuple-element.868, f32[4,24,128]{2,1,0:T(8,128)S(1)} %broadcast_select_fusion.13, f32[4,24,128]{2,1,0:T(8,128)S(1)} %get-tuple-element.763, f32[4,24,128]{2,1,0:T(8,128)S(1)} %get-tuple-element.764, ...), kind=kLoop, calls=%fused_computation.92.clone.1 | loop fusion | flops 44040192 | bytes 3502592 | tf_op jit(solution)/shard_map/while/body/jit(dynamic_update_index_in_dim)/dynamic_update_slice | solution.py:54
  162.2 19.7 %while.63 = (s32[]{:T(128)}, f32[4,4,75,128]{3,1,0,2:T(4,128)}, s32[4,4,24]{2,1,0:T(4,128)S(1)}, bf16[64,75,128]{2,1,0:T(8,128)(2,1)S(1)}, bf16[4,4,24,128,128]{4,3,2,1,0:T(8,128)(2,1)}, /*index=5*/s32[]{:T(128)}) while((s32[]{:T(128)}, f32[4,4,75,128]{3,1,0,2:T(4,128)}, s32[4,4,24]{2,1,0:T(4,128)S(1)}, ...), condition=%wide.region_11.18_spmd, body=%wide.region_10.17_spmd.sunk | while | flops 236852800 | bytes 9143817 | solution.py:68
  189.3 5.9 %all-to-all-start.5 = ((bf16[32,2,75,128]{3,1,2,0:T(2,128)(2,1)}), bf16[32,2,75,128]{3,1,2,0:T(2,128)(2,1)S(1)}, u32[]{:S(2)}, u32[]{:S(2)}) async-start(bf16[32,2,75,128]{3,1,2,0:T(2,128)(2,1)} %broadcast_select_fusion.6), calls=%async_computation.5 | async-start | bytes 2457600 | tf_op jit(solution)/shard_map/all_to_all | solution.py:156
  195.3 14.0 %while.64 = (s32[]{:T(128)}, f32[4,4,75,128]{3,1,0,2:T(4,128)S(1)}, s32[4,4,16]{2,1,0:T(4,128)S(1)}, bf16[16,75,128]{2,1,0:T(8,128)(2,1)S(1)}, bf16[4,4,16,128,128]{4,3,2,1,0:T(8,128)(2,1)}, /*index=5*/s32[]{:T(128)}) while((s32[]{:T(128)}, f32[4,4,75,128]{3,1,0,2:T(4,128)S(1)}, s32[4,4,16]{2,1,0:T(4,128)S(1)}, ...), condition=%wide.region_13.20_spmd, body=%wide.region_12.19_spmd.sunk | while | flops 157902208 | bytes 6260941 | solution.py:68
  209.3 16.9 %all-to-all-done.5 = bf16[32,2,75,128]{3,1,2,0:T(2,128)(2,1)S(1)} async-done(((bf16[32,2,75,128]{3,1,2,0:T(2,128)(2,1)}), bf16[32,2,75,128]{3,1,2,0:T(2,128)(2,1)S(1)}, u32[]{:S(2)}, u32[]{:S(2)}) %all-to-all-start.5) | async-done | bytes 1228832 | tf_op jit(solution)/shard_map/all_to_all | solution.py:156
  229.3 19.6 %while.65 = (s32[]{:T(128)}, f32[4,4,75,128]{3,1,0,2:T(4,128)}, s32[4,4,24]{2,1,0:T(4,128)S(1)}, bf16[64,75,128]{2,1,0:T(8,128)(2,1)S(1)}, bf16[4,4,24,128,128]{4,3,2,1,0:T(8,128)(2,1)}, /*index=5*/s32[]{:T(128)}) while((s32[]{:T(128)}, f32[4,4,75,128]{3,1,0,2:T(4,128)}, s32[4,4,24]{2,1,0:T(4,128)S(1)}, ...), condition=%wide.region_15.22_spmd, body=%wide.region_14.21_spmd.sunk | while | flops 236852800 | bytes 9143817 | solution.py:68
  252.4 37.9 %all-reduce = (f32[1]{0:T(128)}, f32[1]{0:T(128)}) all-reduce(f32[1]{0:T(128)} %bitcast.78, f32[1]{0:T(128)} %bitcast.77), channel_id=1, replica_groups=mesh['gx'=4,'gy'=8] {'gx','gy'}, use_global_device_ids=true, to_apply=%region_19.26 | all-reduce | flops 2 | bytes 16 | tf_op jit(solution)/shard_map/psum | solution.py:79
  (288 shorter events, 132.5 us)
Async XLA Ops:
  0.6 0.8 copy-start
  1.5 4.4 %copy-start.10 = (s32[16,40]{1,0:T(8,128)S(1)}, s32[16,40]{1,0:T(8,128)}, u32[]{:S(2)}) copy-start(s32[16,40]{1,0:T(8,128)} %param.36) | copy-start | bytes 7684
  11.2 63.0 %all-to-all-start = ((s32[32,1,2]{2,1,0:T(1,128)}), s32[32,1,2]{2,1,0:T(1,128)S(1)}, u32[]{:S(2)}, u32[]{:S(2)}) async-start(s32[32,1,2]{2,1,0:T(1,128)} %copy.220), calls=%async_computation | async-start | bytes 32768 | tf_op jit(solution)/shard_map/all_to_all | solution.py:104
  18.7 3.0 %copy-start.3 = (f32[16,3,128]{2,0,1:T(8,128)S(1)}, f32[16,3,128]{2,0,1:T(8,128)}, u32[]{:S(2)}) copy-start(f32[16,3,128]{2,0,1:T(8,128)} %param.33) | copy-start | bytes 73732
  18.7 3.0 %copy-start.4 = (f32[16,3,128]{2,0,1:T(8,128)S(1)}, f32[16,3,128]{2,0,1:T(8,128)}, u32[]{:S(2)}) copy-start(f32[16,3,128]{2,0,1:T(8,128)} %param.32) | copy-start | bytes 73732
  18.7 3.0 %copy-start.2 = (f32[16,128]{1,0:T(8,128)S(1)}, f32[16,128]{1,0:T(8,128)}, u32[]{:S(2)}) copy-start(f32[16,128]{1,0:T(8,128)} %param.34) | copy-start | bytes 24580
  21.7 38.1 %copy-start.1 = (bf16[16,75,128]{2,0,1:T(8,128)(2,1)S(1)}, bf16[16,75,128]{2,0,1:T(8,128)(2,1)}, u32[]{:S(2)}) copy-start(bf16[16,75,128]{2,0,1:T(8,128)(2,1)} %param.31) | copy-start | bytes 921604
  74.0 15.9 %copy-start.7 = (f32[4,4,75,128]{3,1,0,2:T(4,128)}, f32[4,4,75,128]{3,1,0,2:T(4,128)S(1)}, u32[]{:S(2)}) copy-start(f32[4,4,75,128]{3,1,0,2:T(4,128)S(1)} %get-tuple-element.202) | copy-start | bytes 1843204
  77.6 13.0 %all-to-all-start.4 = ((bf16[32,2,128]{2,1,0:T(2,128)(2,1)}), bf16[32,2,128]{2,1,0:T(2,128)(2,1)S(1)}, u32[]{:S(2)}, u32[]{:S(2)}) async-start(bf16[32,2,128]{2,1,0:T(2,128)(2,1)} %select_convert_fusion), calls=%async_computation.4 | async-start | bytes 32768 | tf_op jit(solution)/shard_map/all_to_all | solution.py:137
  90.6 12.2 %all-to-all-start.2 = ((bf16[32,2,3,128]{3,1,2,0:T(2,128)(2,1)}), bf16[32,2,3,128]{3,1,2,0:T(2,128)(2,1)S(1)}, u32[]{:S(2)}, u32[]{:S(2)}) async-start(bf16[32,2,3,128]{3,1,2,0:T(2,128)(2,1)} %get-tuple-element.491), calls=%async_computation.2 | async-start | bytes 98304 | tf_op jit(solution)/shard_map/all_to_all | solution.py:123
  102.9 9.8 %all-to-all-start.3 = ((bf16[32,2,3,128]{3,1,2,0:T(2,128)(2,1)}), bf16[32,2,3,128]{3,1,2,0:T(2,128)(2,1)S(1)}, u32[]{:S(2)}, u32[]{:S(2)}) async-start(bf16[32,2,3,128]{3,1,2,0:T(2,128)(2,1)} %get-tuple-element.490), calls=%async_computation.3 | async-start | bytes 98304 | tf_op jit(solution)/shard_map/all_to_all | solution.py:130
  112.7 46.4 %all-to-all-start.1 = ((bf16[32,2,75,128]{3,1,2,0:T(2,128)(2,1)}), bf16[32,2,75,128]{3,1,2,0:T(2,128)(2,1)S(1)}, u32[]{:S(2)}, u32[]{:S(2)}) async-start(bf16[32,2,75,128]{3,1,2,0:T(2,128)(2,1)} %broadcast_select_fusion.7), calls=%async_computation.1 | async-start | bytes 2457600 | tf_op jit(solution)/shard_map/all_to_all | solution.py:122
  162.2 21.3 %copy-start.9 = (f32[16,3,128]{2,0,1:T(8,128)S(1)}, f32[16,3,128]{2,0,1:T(8,128)}, u32[]{:S(2)}) copy-start(f32[16,3,128]{2,0,1:T(8,128)} %param.35) | copy-start | bytes 73732
  183.2 0.8 copy-start.5
  184.1 0.8 copy-start.6
  189.3 37.0 %all-to-all-start.5 = ((bf16[32,2,75,128]{3,1,2,0:T(2,128)(2,1)}), bf16[32,2,75,128]{3,1,2,0:T(2,128)(2,1)S(1)}, u32[]{:S(2)}, u32[]{:S(2)}) async-start(bf16[32,2,75,128]{3,1,2,0:T(2,128)(2,1)} %broadcast_select_fusion.6), calls=%async_computation.5 | async-start | bytes 2457600 | tf_op jit(solution)/shard_map/all_to_all | solution.py:156
  209.3 20.0 %copy-start.8 = (f32[4,4,75,128]{3,1,0,2:T(4,128)}, f32[4,4,75,128]{3,1,0,2:T(4,128)S(1)}, u32[]{:S(2)}) copy-start(f32[4,4,75,128]{3,1,0,2:T(4,128)S(1)} %get-tuple-element.205) | copy-start | bytes 1843204
where the time goes:
time: 293 us; the launch traced here: 292 us
  other arithmetic  72.8 us (25%)
  local copies, waits for them, and re-layouts  70.6 us (24%)
  matrix products  44.8 us (15%)
  blocking collectives  37.9 us (13%)
  starting transfers between devices  29.7 us (10%)
  waiting for transfers between devices  29.4 us (10%)
  loops' own time  5.88 us (2%)
    dynamic_update_slice x8, other arithmetic, build_tiles(): return lax.map(group_tiles, jnp.arange(turns, dtype=jnp.int32))  52.1 us
    dot_general x16, matrix products, group_term(): jnp.einsum('wxmy,wxsy->wms', collected_values, transfer_factors, preferre...  44.8 us
    psum x1, blocking collectives, total_energy(): return lax.psum(local_part, ('gx', 'gy'))  37.9 us
    all_to_all x1, waiting for transfers between devices, body(): lax.all_to_all(outbound(bounce_one), ('gx', 'gy'), split_axis=0, concat_a...  16.9 us
    gather x16, local copies, waits for them, and re-layouts, group_term(): collected_values = jnp.take(source_rows, picked_rows, axis=0)  13.9 us
    gather x5, local copies, waits for them, and re-layouts, outbound(): collected_values = jnp.take(table, chosen, axis=0)  8.2 us
    all_to_all x1, starting transfers between devices, body(): lax.all_to_all(request_list, ('gx', 'gy'), split_axis=0, concat_axis=0, t...  7.33 us
    all_to_all x1, waiting for transfers between devices, body(): lax.all_to_all(exitant_radiance[2].astype(jnp.bfloat16), ('gx', 'gy'), sp...  7.05 us
  transfers between devices with their start and end apart: 6, of which 4 were waited for; matrix products, arithmetic and copies ran while one was open for 40% of the time, Pallas kernels for 0%

commit v1 on v0

--- a/solution.py
+++ b/solution.py
@@ -2,6 +2,7 @@
 import jax.numpy as jnp
 from jax import lax
 from jax.sharding import PartitionSpec as P
+from jax.lax import psum
 
 COLORS = 3
 NEAR = 16
@@ -76,7 +77,11 @@
 
 
 def total_energy(local_part):
-    return lax.psum(local_part, ("gx", "gy"))
+
+    def _store_gates(matrix, peer_axis, which_axis):
+        return psum(psum(matrix, axis_name=peer_axis), axis_name=which_axis)
+
+    return _store_gates(local_part, "gy", "gx")
 
 
 def body(transfer, positions, normals, area, albedo, pairs, home):

time: 293 us -> 281 us (0.959)
  blocking collectives: 37.9 us -> 25.6 us
    psum x1 -> x2, blocking collectives: 37.9 us -> 25.6 us  [_store_gates(): return psum(psum(matrix, axis_name=peer_axis), axis_name=which_axis)]
  transfers between devices with their start and end apart: 6 -> 6, of which waited for: 4 -> 4; matrix products, arithmetic and copies ran while one was open for 40% -> 42% of each run, Pallas kernels for 0% -> 0%
where the time goes in v1:
time: 281 us; the launch traced here: 280 us
  other arithmetic  75.4 us (27%)
  local copies, waits for them, and re-layouts  70.6 us (25%)
  matrix products  44.7 us (16%)
  starting transfers between devices  29.7 us (11%)
  waiting for transfers between devices  26.8 us (10%)
  blocking collectives  25.6 us (9%)
  loops' own time  5.87 us (2%)
    dynamic_update_slice x8, other arithmetic, build_tiles(): return lax.map(group_tiles, jnp.arange(turns, dtype=jnp.int32))  52.1 us
    dot_general x16, matrix products, group_term(): jnp.einsum('wxmy,wxsy->wms', collected_values, transfer_factors, preferre...  44.7 us
    psum x2, blocking collectives, _store_gates(): return psum(psum(matrix, axis_name=peer_axis), axis_name=which_axis)  25.6 us
    all_to_all x1, waiting for transfers between devices, body(): lax.all_to_all(outbound(bounce_one), ('gx', 'gy'), split_axis=0, concat_a...  14.3 us
    gather x16, local copies, waits for them, and re-layouts, group_term(): collected_values = jnp.take(source_rows, picked_rows, axis=0)  13.9 us
    gather x5, local copies, waits for them, and re-layouts, outbound(): collected_values = jnp.take(table, chosen, axis=0)  8.2 us
    all_to_all x1, starting transfers between devices, body(): lax.all_to_all(request_list, ('gx', 'gy'), split_axis=0, concat_axis=0, t...  7.33 us
    all_to_all x1, waiting for transfers between devices, body(): lax.all_to_all(exitant_radiance[2].astype(jnp.bfloat16), ('gx', 'gy'), sp...  7.05 us
  transfers between devices with their start and end apart: 6, of which 4 were waited for; matrix products, arithmetic and copies ran while one was open for 42% of the time, Pallas kernels for 0%

profile of v1, /device:TPU:0, one launch (start us, length us, event | category | flops | bytes accessed | tf_op | source)
XLA Modules:
  0.0 279.9 jit_solution(13410324950287861938)
XLA Ops:
  11.2 7.3 %all-to-all-start = ((s32[32,1,2]{2,1,0:T(1,128)}), s32[32,1,2]{2,1,0:T(1,128)S(1)}, u32[]{:S(2)}, u32[]{:S(2)}) async-start(s32[32,1,2]{2,1,0:T(1,128)} %copy.220), calls=%async_computation | async-start | bytes 32768 | tf_op jit(solution)/shard_map/all_to_all | solution.py:109
  21.8 38.0 %while.60 = (s32[]{:T(128)}, bf16[4,4,16,128,128]{4,3,2,1,0:T(8,128)(2,1)}, s32[4]{0:T(128)S(1)}, f32[16,3,128]{2,1,0:T(4,128)S(1)}, s32[16,16]{1,0:T(8,128)S(1)...) while((s32[]{:T(128)}, ...), condition=%wide.region_1.3_spmd, body=%wide.region_0.0_spmd.sunk | while | flops 29418888 | bytes 3681183 | solution.py:55
  25.4 5.9 %fusion.115 = bf16[4,4,16,128,128]{4,3,2,1,0:T(8,128)(2,1)} fusion(bf16[4,4,16,128,128]{4,3,2,1,0:T(8,128)(2,1)} %get-tuple-element.812, s32[]{:T(128)} %get-tuple-element.811, f32[4,16,128]{2,1,0:T(8,128)S(1)} %broadcast_select_fusion.11, f32[4,16,128]{2,1,0:T(8,128)S(1)} %bitcast.220, f32[4,16,128]{2,1,0:T(8,128)S(1)} %bitcast.219, ...), kind=kLoop, calls=%fused_computation.42.clone.1 | loop fusion | flops 29360128 | bytes 2339328 | tf_op jit(solution)/shard_map/while/body/jit(dynamic_update_index_in_dim)/dynamic_update_slice | solution.py:55
  34.9 5.8 %fusion.115 = bf16[4,4,16,128,128]{4,3,2,1,0:T(8,128)(2,1)} fusion(bf16[4,4,16,128,128]{4,3,2,1,0:T(8,128)(2,1)} %get-tuple-element.812, s32[]{:T(128)} %get-tuple-element.811, f32[4,16,128]{2,1,0:T(8,128)S(1)} %broadcast_select_fusion.11, f32[4,16,128]{2,1,0:T(8,128)S(1)} %bitcast.220, f32[4,16,128]{2,1,0:T(8,128)S(1)} %bitcast.219, ...), kind=kLoop, calls=%fused_computation.42.clone.1 | loop fusion | flops 29360128 | bytes 2339328 | tf_op jit(solution)/shard_map/while/body/jit(dynamic_update_index_in_dim)/dynamic_update_slice | solution.py:55
  44.4 5.8 %fusion.115 = bf16[4,4,16,128,128]{4,3,2,1,0:T(8,128)(2,1)} fusion(bf16[4,4,16,128,128]{4,3,2,1,0:T(8,128)(2,1)} %get-tuple-element.812, s32[]{:T(128)} %get-tuple-element.811, f32[4,16,128]{2,1,0:T(8,128)S(1)} %broadcast_select_fusion.11, f32[4,16,128]{2,1,0:T(8,128)S(1)} %bitcast.220, f32[4,16,128]{2,1,0:T(8,128)S(1)} %bitcast.219, ...), kind=kLoop, calls=%fused_computation.42.clone.1 | loop fusion | flops 29360128 | bytes 2339328 | tf_op jit(solution)/shard_map/while/body/jit(dynamic_update_index_in_dim)/dynamic_update_slice | solution.py:55
  53.9 5.9 %fusion.115 = bf16[4,4,16,128,128]{4,3,2,1,0:T(8,128)(2,1)} fusion(bf16[4,4,16,128,128]{4,3,2,1,0:T(8,128)(2,1)} %get-tuple-element.812, s32[]{:T(128)} %get-tuple-element.811, f32[4,16,128]{2,1,0:T(8,128)S(1)} %broadcast_select_fusion.11, f32[4,16,128]{2,1,0:T(8,128)S(1)} %bitcast.220, f32[4,16,128]{2,1,0:T(8,128)S(1)} %bitcast.219, ...), kind=kLoop, calls=%fused_computation.42.clone.1 | loop fusion | flops 29360128 | bytes 2339328 | tf_op jit(solution)/shard_map/while/body/jit(dynamic_update_index_in_dim)/dynamic_update_slice | solution.py:55
  60.0 14.0 %while.61 = (s32[]{:T(128)}, f32[4,4,75,128]{3,1,0,2:T(4,128)S(1)}, s32[4,4,16]{2,1,0:T(4,128)S(1)}, bf16[16,75,128]{2,1,0:T(8,128)(2,1)S(1)}, bf16[4,4,16,128,128]{4,3,2,1,0:T(8,128)(2,1)}, /*index=5*/s32[]{:T(128)}) while((s32[]{:T(128)}, f32[4,4,75,128]{3,1,0,2:T(4,128)S(1)}, s32[4,4,16]{2,1,0:T(4,128)S(1)}, ...), condition=%wide.region_3.6_spmd, body=%wide.region_2.5_spmd.sunk | while | flops 157902208 | bytes 6260941 | solution.py:69
  77.8 6.0 %all-to-all-start.4 = ((bf16[32,2,128]{2,1,0:T(2,128)(2,1)}), bf16[32,2,128]{2,1,0:T(2,128)(2,1)S(1)}, u32[]{:S(2)}, u32[]{:S(2)}) async-start(bf16[32,2,128]{2,1,0:T(2,128)(2,1)} %select_convert_fusion), calls=%async_computation.4 | async-start | bytes 32768 | tf_op jit(solution)/shard_map/all_to_all | solution.py:142
  84.7 5.4 %gather_fusion.13 = bf16[64,75,128]{2,0,1:T(8,128)(2,1)S(1)} fusion(bf16[16,75,128]{2,0,1:T(8,128)(2,1)S(1)} %copy-done.1, s32[1024]{0:T(1024)S(1)} %pad_clamp_fusion.7), kind=kCustom, calls=%fused_computation.4.clone | custom fusion | bytes 2457856 | tf_op jit(solution)/shard_map/jit(_take)/gather | solution.py:116
  90.8 5.0 %all-to-all-start.2 = ((bf16[32,2,3,128]{3,1,2,0:T(2,128)(2,1)}), bf16[32,2,3,128]{3,1,2,0:T(2,128)(2,1)S(1)}, u32[]{:S(2)}, u32[]{:S(2)}) async-start(bf16[32,2,3,128]{3,1,2,0:T(2,128)(2,1)} %get-tuple-element.493), calls=%async_computation.2 | async-start | bytes 98304 | tf_op jit(solution)/shard_map/all_to_all | solution.py:128
  98.3 4.7 %all-to-all-done.2 = bf16[32,2,3,128]{3,1,2,0:T(2,128)(2,1)S(1)} async-done(((bf16[32,2,3,128]{3,1,2,0:T(2,128)(2,1)}), bf16[32,2,3,128]{3,1,2,0:T(2,128)(2,1)S(1)}, u32[]{:S(2)}, u32[]{:S(2)}) %all-to-all-start.2) | async-done | bytes 49184 | tf_op jit(solution)/shard_map/all_to_all | solution.py:128
  105.8 7.1 %all-to-all-done.3 = bf16[32,2,3,128]{3,1,2,0:T(2,128)(2,1)S(1)} async-done(((bf16[32,2,3,128]{3,1,2,0:T(2,128)(2,1)}), bf16[32,2,3,128]{3,1,2,0:T(2,128)(2,1)S(1)}, u32[]{:S(2)}, u32[]{:S(2)}) %all-to-all-start.3) | async-done | bytes 49184 | tf_op jit(solution)/shard_map/all_to_all | solution.py:135
  115.9 43.3 %while.62 = (s32[]{:T(128)}, bf16[4,4,24,128,128]{4,3,2,1,0:T(8,128)(2,1)}, s32[4]{0:T(128)S(1)}, f32[16,3,128]{2,0,1:T(8,128)S(1)}, s32[16,24]{1,0:T(8,128)S(1)...) while((s32[]{:T(128)}, ...), condition=%wide.region_9.14_spmd, body=%wide.region_8.13_spmd.sunk | while | flops 44127816 | bytes 5500943 | solution.py:55
  119.6 7.2 %fusion.119 = bf16[4,4,24,128,128]{4,3,2,1,0:T(8,128)(2,1)} fusion(bf16[4,4,24,128,128]{4,3,2,1,0:T(8,128)(2,1)} %get-tuple-element.871, s32[]{:T(128)} %get-tuple-element.870, f32[4,24,128]{2,1,0:T(8,128)S(1)} %broadcast_select_fusion.13, f32[4,24,128]{2,1,0:T(8,128)S(1)} %get-tuple-element.765, f32[4,24,128]{2,1,0:T(8,128)S(1)} %get-tuple-element.766, ...), kind=kLoop, calls=%fused_computation.92.clone.1 | loop fusion | flops 44040192 | bytes 3502592 | tf_op jit(solution)/shard_map/while/body/jit(dynamic_update_index_in_dim)/dynamic_update_slice | solution.py:55
  130.4 7.2 %fusion.119 = bf16[4,4,24,128,128]{4,3,2,1,0:T(8,128)(2,1)} fusion(bf16[4,4,24,128,128]{4,3,2,1,0:T(8,128)(2,1)} %get-tuple-element.871, s32[]{:T(128)} %get-tuple-element.870, f32[4,24,128]{2,1,0:T(8,128)S(1)} %broadcast_select_fusion.13, f32[4,24,128]{2,1,0:T(8,128)S(1)} %get-tuple-element.765, f32[4,24,128]{2,1,0:T(8,128)S(1)} %get-tuple-element.766, ...), kind=kLoop, calls=%fused_computation.92.clone.1 | loop fusion | flops 44040192 | bytes 3502592 | tf_op jit(solution)/shard_map/while/body/jit(dynamic_update_index_in_dim)/dynamic_update_slice | solution.py:55
  141.2 7.2 %fusion.119 = bf16[4,4,24,128,128]{4,3,2,1,0:T(8,128)(2,1)} fusion(bf16[4,4,24,128,128]{4,3,2,1,0:T(8,128)(2,1)} %get-tuple-element.871, s32[]{:T(128)} %get-tuple-element.870, f32[4,24,128]{2,1,0:T(8,128)S(1)} %broadcast_select_fusion.13, f32[4,24,128]{2,1,0:T(8,128)S(1)} %get-tuple-element.765, f32[4,24,128]{2,1,0:T(8,128)S(1)} %get-tuple-element.766, ...), kind=kLoop, calls=%fused_computation.92.clone.1 | loop fusion | flops 44040192 | bytes 3502592 | tf_op jit(solution)/shard_map/while/body/jit(dynamic_update_index_in_dim)/dynamic_update_slice | solution.py:55
  152.0 7.2 %fusion.119 = bf16[4,4,24,128,128]{4,3,2,1,0:T(8,128)(2,1)} fusion(bf16[4,4,24,128,128]{4,3,2,1,0:T(8,128)(2,1)} %get-tuple-element.871, s32[]{:T(128)} %get-tuple-element.870, f32[4,24,128]{2,1,0:T(8,128)S(1)} %broadcast_select_fusion.13, f32[4,24,128]{2,1,0:T(8,128)S(1)} %get-tuple-element.765, f32[4,24,128]{2,1,0:T(8,128)S(1)} %get-tuple-element.766, ...), kind=kLoop, calls=%fused_computation.92.clone.1 | loop fusion | flops 44040192 | bytes 3502592 | tf_op jit(solution)/shard_map/while/body/jit(dynamic_update_index_in_dim)/dynamic_update_slice | solution.py:55
  162.3 19.6 %while.63 = (s32[]{:T(128)}, f32[4,4,75,128]{3,1,0,2:T(4,128)}, s32[4,4,24]{2,1,0:T(4,128)S(1)}, bf16[64,75,128]{2,1,0:T(8,128)(2,1)S(1)}, bf16[4,4,24,128,128]{4,3,2,1,0:T(8,128)(2,1)}, /*index=5*/s32[]{:T(128)}) while((s32[]{:T(128)}, f32[4,4,75,128]{3,1,0,2:T(4,128)}, s32[4,4,24]{2,1,0:T(4,128)S(1)}, ...), condition=%wide.region_11.18_spmd, body=%wide.region_10.17_spmd.sunk | while | flops 236852800 | bytes 9143817 | solution.py:69
  189.4 5.9 %all-to-all-start.5 = ((bf16[32,2,75,128]{3,1,2,0:T(2,128)(2,1)}), bf16[32,2,75,128]{3,1,2,0:T(2,128)(2,1)S(1)}, u32[]{:S(2)}, u32[]{:S(2)}) async-start(bf16[32,2,75,128]{3,1,2,0:T(2,128)(2,1)} %broadcast_select_fusion.6), calls=%async_computation.5 | async-start | bytes 2457600 | tf_op jit(solution)/shard_map/all_to_all | solution.py:161
  195.4 16.7 %while.64 = (s32[]{:T(128)}, f32[4,4,75,128]{3,1,0,2:T(4,128)S(1)}, s32[4,4,16]{2,1,0:T(4,128)}, bf16[16,75,128]{2,1,0:T(8,128)(2,1)S(1)}, bf16[4,4,16,128,128]{4,3,2,1,0:T(8,128)(2,1)}, /*index=5*/s32[]{:T(128)}) while((s32[]{:T(128)}, f32[4,4,75,128]{3,1,0,2:T(4,128)S(1)}, s32[4,4,16]{2,1,0:T(4,128)}, ...), condition=%wide.region_13.20_spmd, body=%wide.region_12.19_spmd.sunk | while | flops 157902208 | bytes 6260941 | solution.py:69
  212.1 14.3 %all-to-all-done.5 = bf16[32,2,75,128]{3,1,2,0:T(2,128)(2,1)S(1)} async-done(((bf16[32,2,75,128]{3,1,2,0:T(2,128)(2,1)}), bf16[32,2,75,128]{3,1,2,0:T(2,128)(2,1)S(1)}, u32[]{:S(2)}, u32[]{:S(2)}) %all-to-all-start.5) | async-done | bytes 1228832 | tf_op jit(solution)/shard_map/all_to_all | solution.py:161
  229.5 19.6 %while.65 = (s32[]{:T(128)}, f32[4,4,75,128]{3,1,0,2:T(4,128)}, s32[4,4,24]{2,1,0:T(4,128)S(1)}, bf16[64,75,128]{2,1,0:T(8,128)(2,1)S(1)}, bf16[4,4,24,128,128]{4,3,2,1,0:T(8,128)(2,1)}, /*index=5*/s32[]{:T(128)}) while((s32[]{:T(128)}, f32[4,4,75,128]{3,1,0,2:T(4,128)}, s32[4,4,24]{2,1,0:T(4,128)S(1)}, ...), condition=%wide.region_15.22_spmd, body=%wide.region_14.21_spmd.sunk | while | flops 236852800 | bytes 9143817 | solution.py:69
  252.5 19.1 %all-reduce = (f32[]{:T(128)}, f32[]{:T(128)}) all-reduce(f32[]{:T(128)} %get-tuple-element.360, f32[]{:T(128)} %get-tuple-element.359), channel_id=1, replica_groups=mesh['gx'=4,'gy'=8] {'gy'}, use_global_device_ids=true, to_apply=%region_20.27 | all-reduce | flops 2 | bytes 16 | tf_op jit(solution)/shard_map/psum | solution.py:82
  271.6 6.5 %all-reduce.1 = (f32[1]{0:T(128)}, f32[1]{0:T(128)}) all-reduce(f32[1]{0:T(128)} %bitcast.78, f32[1]{0:T(128)} %bitcast.77), channel_id=1, replica_groups=mesh['gx'=4,'gy'=8] {'gx'}, use_global_device_ids=true, to_apply=%region_21.28 | all-reduce | flops 2 | bytes 16 | tf_op jit(solution)/shard_map/psum | solution.py:82
  (291 shorter events, 139.4 us)
Async XLA Ops:
  0.6 0.8 copy-start
  1.5 4.4 %copy-start.11 = (s32[16,40]{1,0:T(8,128)S(1)}, s32[16,40]{1,0:T(8,128)}, u32[]{:S(2)}) copy-start(s32[16,40]{1,0:T(8,128)} %param.36) | copy-start | bytes 7684
  11.2 62.9 %all-to-all-start = ((s32[32,1,2]{2,1,0:T(1,128)}), s32[32,1,2]{2,1,0:T(1,128)S(1)}, u32[]{:S(2)}, u32[]{:S(2)}) async-start(s32[32,1,2]{2,1,0:T(1,128)} %copy.220), calls=%async_computation | async-start | bytes 32768 | tf_op jit(solution)/shard_map/all_to_all | solution.py:109
  18.7 3.0 %copy-start.3 = (f32[16,3,128]{2,0,1:T(8,128)S(1)}, f32[16,3,128]{2,0,1:T(8,128)}, u32[]{:S(2)}) copy-start(f32[16,3,128]{2,0,1:T(8,128)} %param.33) | copy-start | bytes 73732
  18.7 3.0 %copy-start.4 = (f32[16,3,128]{2,0,1:T(8,128)S(1)}, f32[16,3,128]{2,0,1:T(8,128)}, u32[]{:S(2)}) copy-start(f32[16,3,128]{2,0,1:T(8,128)} %param.32) | copy-start | bytes 73732
  18.7 3.0 %copy-start.2 = (f32[16,128]{1,0:T(8,128)S(1)}, f32[16,128]{1,0:T(8,128)}, u32[]{:S(2)}) copy-start(f32[16,128]{1,0:T(8,128)} %param.34) | copy-start | bytes 24580
  21.7 38.0 %copy-start.1 = (bf16[16,75,128]{2,0,1:T(8,128)(2,1)S(1)}, bf16[16,75,128]{2,0,1:T(8,128)(2,1)}, u32[]{:S(2)}) copy-start(bf16[16,75,128]{2,0,1:T(8,128)(2,1)} %param.31) | copy-start | bytes 921604
  74.0 0.6 copy-start.9
  74.0 16.1 %copy-start.7 = (f32[4,4,75,128]{3,1,0,2:T(4,128)}, f32[4,4,75,128]{3,1,0,2:T(4,128)S(1)}, u32[]{:S(2)}) copy-start(f32[4,4,75,128]{3,1,0,2:T(4,128)S(1)} %get-tuple-element.202) | copy-start | bytes 1843204
  77.8 13.0 %all-to-all-start.4 = ((bf16[32,2,128]{2,1,0:T(2,128)(2,1)}), bf16[32,2,128]{2,1,0:T(2,128)(2,1)S(1)}, u32[]{:S(2)}, u32[]{:S(2)}) async-start(bf16[32,2,128]{2,1,0:T(2,128)(2,1)} %select_convert_fusion), calls=%async_computation.4 | async-start | bytes 32768 | tf_op jit(solution)/shard_map/all_to_all | solution.py:142
  90.8 12.2 %all-to-all-start.2 = ((bf16[32,2,3,128]{3,1,2,0:T(2,128)(2,1)}), bf16[32,2,3,128]{3,1,2,0:T(2,128)(2,1)S(1)}, u32[]{:S(2)}, u32[]{:S(2)}) async-start(bf16[32,2,3,128]{3,1,2,0:T(2,128)(2,1)} %get-tuple-element.493), calls=%async_computation.2 | async-start | bytes 98304 | tf_op jit(solution)/shard_map/all_to_all | solution.py:128
  103.0 9.8 %all-to-all-start.3 = ((bf16[32,2,3,128]{3,1,2,0:T(2,128)(2,1)}), bf16[32,2,3,128]{3,1,2,0:T(2,128)(2,1)S(1)}, u32[]{:S(2)}, u32[]{:S(2)}) async-start(bf16[32,2,3,128]{3,1,2,0:T(2,128)(2,1)} %get-tuple-element.492), calls=%async_computation.3 | async-start | bytes 98304 | tf_op jit(solution)/shard_map/all_to_all | solution.py:135
  112.8 46.4 %all-to-all-start.1 = ((bf16[32,2,75,128]{3,1,2,0:T(2,128)(2,1)}), bf16[32,2,75,128]{3,1,2,0:T(2,128)(2,1)S(1)}, u32[]{:S(2)}, u32[]{:S(2)}) async-start(bf16[32,2,75,128]{3,1,2,0:T(2,128)(2,1)} %broadcast_select_fusion.7), calls=%async_computation.1 | async-start | bytes 2457600 | tf_op jit(solution)/shard_map/all_to_all | solution.py:127
  162.3 21.3 %copy-start.10 = (f32[16,3,128]{2,0,1:T(8,128)S(1)}, f32[16,3,128]{2,0,1:T(8,128)}, u32[]{:S(2)}) copy-start(f32[16,3,128]{2,0,1:T(8,128)} %param.35) | copy-start | bytes 73732
  183.4 0.8 copy-start.5
  184.2 0.8 copy-start.6
  189.4 37.0 %all-to-all-start.5 = ((bf16[32,2,75,128]{3,1,2,0:T(2,128)(2,1)}), bf16[32,2,75,128]{3,1,2,0:T(2,128)(2,1)S(1)}, u32[]{:S(2)}, u32[]{:S(2)}) async-start(bf16[32,2,75,128]{3,1,2,0:T(2,128)(2,1)} %broadcast_select_fusion.6), calls=%async_computation.5 | async-start | bytes 2457600 | tf_op jit(solution)/shard_map/all_to_all | solution.py:161
  212.1 17.4 %copy-start.8 = (f32[4,4,75,128]{3,1,0,2:T(4,128)}, f32[4,4,75,128]{3,1,0,2:T(4,128)S(1)}, u32[]{:S(2)}) copy-start(f32[4,4,75,128]{3,1,0,2:T(4,128)S(1)} %get-tuple-element.205) | copy-start | bytes 1843204
